TPU v7x, 32 devices: a whole 2x2x4 slice. The times are simulated.
32 devices in a mesh: gx: 16 (over z, y, x), gy: 2 (over core).
Axes of the slice: x: 2, y: 2, z: 4, core: 2. Of those that a mesh axis runs over, the one named last changes fastest.
Arguments:
- droplets: float32 [2, 32, 32, 1024], P(None, None, 'gx', 'gy'), as said below
- moves: int32 [2, 32, 32, 1024], P(None, None, 'gx', 'gy'), may hold values from 0 to 8, as said below
- pairing: int32 [2, 32, 32, 1024], P(None, None, 'gx', 'gy'), may hold values from 0 to 31, as said below
- collisions: int32 [2, 16, 32, 1024], P(None, None, 'gx', 'gy'), may hold values from 0 to 3
Outputs:
- droplets_out: float32 [2, 32, 32, 1024], P(None, None, 'gx', 'gy')
- moments: float32 [2, 2, 16], replicated
Inputs may be any that keep to these rules, and one draw needn't show every extreme that they name: `droplets`: entry 0 holds whole-number multiplicities from 24 to below 300, entry 1 masses from 0.05 to 2. `moves`: A code c means a step of c // 3 - 1 along x and c % 3 - 1 along y. In each step, slot and level, all droplets of one y-row take the same x-step and all droplets landing in one x-column take the same y-step, so every cell and slot receives exactly one droplet. `pairing`: for each step and cell, the entries along the slot dimension are a permutation of 0 to 31.
All inputs are finite; a program needn't handle non-finite values.
Results may differ from a plain program's by a relative error of at most 0.0003.
Values sent between devices are 32-bit elements; how exact they have to be, the bound alone decides.
A program may use at most 64 MiB of HBM per device.

v0:
```python
import jax
import jax.numpy as jnp
from jax import lax
from jax.sharding import PartitionSpec as P

LEVELS = 16
count_unit = 4096.0


def padded(array, sides, width):
    for axis, dim in sides:
        size, length = (lax.axis_size(axis), array.shape[dim])
        up = [(i, (i + 1) % size) for i in range(size)]
        down = [(j, i) for i, j in up]
        last = lax.slice_in_dim(array, length - width, length, axis=dim)
        leading = lax.slice_in_dim(array, 0, width, axis=dim)
        before = lax.ppermute(last, axis, up)
        after = lax.ppermute(leading, axis, down)
        array = jnp.concatenate([before, array, after], axis=dim)
    return array


def spread(state, codes):
    twos, slots, cols, rows, levels = state.shape
    extended = jnp.zeros((twos, slots, cols + 2, rows + 2, levels), state.dtype)
    for direction in range(9):
        step_x = direction // 3 - 1
        step_y = direction % 3 - 1
        chosen = jnp.where((codes == direction)[None], state, jnp.zeros_like(state))
        extended = extended + jnp.pad(
            chosen, ((0, 0), (0, 0), (1 + step_x, 1 - step_x), (1 + step_y, 1 - step_y), (0, 0))
        )
    return extended


def settle(extended, cols, rows):
    twos, slots, wide, tall, levels = extended.shape
    rims = jnp.stack([extended[:, :, 0], extended[:, :, cols + 1]], axis=2).reshape(
        twos, slots, 2, (rows + 2) * levels
    )
    got = padded(rims, (("gx", 2),), 1).reshape(twos, slots, 4, rows + 2, levels)
    middle = (
        extended[:, :, 1 : cols + 1]
        .at[:, :, 0]
        .add(got[:, :, 0])
        .at[:, :, cols - 1]
        .add(got[:, :, 3])
    )
    rims = jnp.stack([middle[:, :, :, 0], middle[:, :, :, rows + 1]], axis=2).reshape(
        twos, slots, 2, cols * levels
    )
    got = padded(rims, (("gy", 2),), 1).reshape(twos, slots, 4, cols, levels)
    block = (
        middle[:, :, :, 1 : rows + 1]
        .at[:, :, :, 0]
        .add(got[:, :, 0])
        .at[:, :, :, rows - 1]
        .add(got[:, :, 3])
    )
    return block


def collide(first_count, second_count, first_mass, second_mass, tries):
    big_first = first_count >= second_count
    larger = jnp.where(big_first, first_count, second_count)
    smaller = jnp.where(big_first, second_count, first_count)
    larger_mass = jnp.where(big_first, first_mass, second_mass)
    smaller_mass = jnp.where(big_first, second_mass, first_mass)
    taken = jnp.minimum(tries, larger // smaller)
    remain = larger - taken * smaller
    splits = remain == 0
    halved = smaller // 2
    larger_new = jnp.where(splits, halved, remain)
    smaller_new = jnp.where(splits, smaller - halved, smaller)
    grown = smaller_mass + taken.astype(first_mass.dtype) * larger_mass
    larger_mass_new = jnp.where(splits, grown, larger_mass)
    first_new = jnp.where(big_first, larger_new, smaller_new)
    second_new = jnp.where(big_first, smaller_new, larger_new)
    first_mass_new = jnp.where(big_first, larger_mass_new, grown)
    second_mass_new = jnp.where(big_first, grown, larger_mass_new)
    return (first_new, second_new, first_mass_new, second_mass_new)


def pair_column(counts_f, masses, order, tries):
    slots = counts_f.shape[0]
    slot_ids = lax.broadcasted_iota(jnp.int32, (slots, slots, 1), 1)
    hits = order[:, None, :] == slot_ids
    counts = counts_f.astype(jnp.int32)
    counts_p = jnp.sum(jnp.where(hits, counts[None], 0), axis=1)
    masses_p = jnp.sum(jnp.where(hits, masses[None], jnp.zeros_like(masses)[None]), axis=1)
    first_new, second_new, first_mass, second_mass = collide(
        counts_p[0::2], counts_p[1::2], masses_p[0::2], masses_p[1::2], tries
    )
    counts_pair = jnp.stack([first_new, second_new], axis=1).reshape(counts_p.shape)
    masses_pair = jnp.stack([first_mass, second_mass], axis=1).reshape(masses_p.shape)
    counts_new = jnp.sum(jnp.where(hits, counts_pair[:, None], 0), axis=0)
    masses_new = jnp.sum(
        jnp.where(hits, masses_pair[:, None], jnp.zeros_like(masses_pair)[:, None]), axis=0
    )
    return (counts_new.astype(counts_f.dtype), masses_new)


def coalesce(block, order, tries):
    twos, slots, cols, rows, levels = block.shape
    flat = block.reshape(twos, slots, cols, rows * levels)
    results = []
    for column in range(cols):
        counts_new, masses_new = pair_column(
            flat[0, :, column], flat[1, :, column], order[:, column], tries[:, column]
        )
        results.append(jnp.stack([counts_new, masses_new]))
    return jnp.stack(results, axis=2).reshape(block.shape)


def shards(droplets, moves, pairing, collisions):
    twos, slots, cols, flat = droplets.shape
    levels = LEVELS
    rows = flat // levels
    state = droplets.reshape(twos, slots, cols, rows, levels)
    totals = []
    for step in range(moves.shape[0]):
        codes = moves[step].reshape(slots, cols, rows, levels)
        state = settle(spread(state, codes), cols, rows)
        state = coalesce(state, pairing[step], collisions[step])
        count_sum = jnp.sum(state[0], axis=(0, 1, 2))
        liquid_sum = jnp.sum(state[0] * state[1], axis=(0, 1, 2))
        terms = jnp.stack([count_sum, liquid_sum])
        totals.append(lax.psum(terms, ("gx", "gy")))
    summed = jnp.stack(totals)
    cells_x = cols * lax.axis_size("gx")
    cells_y = rows * lax.axis_size("gy")
    moments = summed / (cells_x * cells_y * count_unit)
    return (state.reshape(droplets.shape), moments)


def solution(mesh):
    placed = (
        P(None, None, "gx", "gy"),
        P(None, None, "gx", "gy"),
        P(None, None, "gx", "gy"),
        P(None, None, "gx", "gy"),
    )
    return jax.shard_map(
        shards,
        mesh=mesh,
        in_specs=placed,
        out_specs=(P(None, None, "gx", "gy"), P()),
        check_vma=False,
    )
```

profile of v0, /device:TPU:0, one launch (start us, length us, event | category | flops | bytes accessed | tf_op | source)
XLA Modules:
  0.0 107.8 jit_solution(15676673924151060772)
XLA Ops:
  0.6 1.0 fusion.55
  1.9 0.8 broadcast_compare_fusion.16
  3.1 1.2 %broadcast_select_fusion.17 = (f32[2,32,2,32,16]{1,4,3,2,0:T(8,128)S(1)}, f32[2,32,2,32,16]{1,4,3,2,0:T(8,128)S(1)}, f32[2,32,2,32,16]{1,4,3,2,0:T(8,128)S(1)}, ...) fusion(f32[2,32,2,32,16]{1,4,3,2,0:T(8,128)S(1)} %bitcast.219, ...), kind=kLoop, calls=%fused_computation.50 | loop fusion | flops 589824 | bytes 2916352 | tf_op jit(solution)/shard_map/jit(_where)/select_n | solution.py:29
  5.2 1.1 %copy.85 = f32[2,32,1,544]{3,1,2,0:T(8,128)} copy(f32[2,32,1,544]{1,3,2,0:T(8,128)S(1)} %get-tuple-element.121) | data formatting | bytes 278528 | tf_op jit(solution)/shard_map/slice | solution.py:15
  6.3 3.0 %collective-permute-start = (f32[2,32,1,544]{3,1,2,0:T(8,128)}, f32[2,32,1,544]{3,1,2,0:T(8,128)}, u32[]{:S(2)}, u32[]{:S(2)}) collective-permute-start(f32[2,32,1,544]{3,1,2,0:T(8,128)} %copy.85), channel_id=1, source_target_pairs={{0,2},{2,4},{4,6},{6,8},{8,10},{10,12},{12,14},{14,16},{16,18},{18... | collective-permute-start | bytes 417800 | tf_op jit(solution)/shard_map/ppermute | solution.py:17
  9.2 0.9 copy.88
  10.1 4.0 %collective-permute-start.1 = (f32[2,32,1,544]{3,1,2,0:T(8,128)}, f32[2,32,1,544]{3,1,2,0:T(8,128)}, u32[]{:S(2)}, u32[]{:S(2)}) collective-permute-start(f32[2,32,1,544]{3,1,2,0:T(8,128)} %copy.88), channel_id=1, source_target_pairs={{2,0},{4,2},{6,4},{8,6},{10,8},{12,10},{14,12},{16,14},{18,16},{20... | collective-permute-start | bytes 417800 | tf_op jit(solution)/shard_map/ppermute | solution.py:18
  14.8 1.0 copy.130
  15.9 2.5 %broadcast_compare_fusion.17 = (pred[1,32,2,512]{1,3,2,0:T(8,128)(4,1)}, pred[1,32,2,512]{1,3,2,0:T(8,128)(4,1)}, pred[1,32,2,512]{1,3,2,0:T(8,128)(4,1)}, pred[...) fusion(s32[1,32,2,512]{1,3,2,0:T(8,128)} %copy.130), kind=kLoop, calls=%fused_computation.87 | loop fusion | flops 294912 | bytes 425984 | tf_op jit(solution)/shard_map/eq | solution.py:29
  18.4 2.0 %fusion.56 = (s32[32,1,512]{2,1,0:T(1,128)}, s32[32,1,512]{2,1,0:T(1,128)}, s32[32,1,512]{2,1,0:T(1,128)}, s32[32,1,512]{2,1,0:T(1,128)}) fusion(s32[32,2,512]{2,1,0:T(2,128)} %get-tuple-element.166, s32[32,2,512]{2,1,0:T(2,128)} %get-tuple-element.167), kind=kLoop, calls=%fused_computation.232 | loop fusion | bytes 524288 | tf_op jit(solution)/shard_map/slice | solution.py:109
  20.4 0.9 fusion.57
  21.3 1.9 %copy.86 = f32[2,32,1,544]{1,3,0,2:T(8,128)} copy(f32[2,32,1,544]{3,1,2,0:T(8,128)} %collective-permute-done) | data formatting | bytes 278528 | tf_op jit(solution)/shard_map/ppermute | solution.py:17
  23.3 1.1 %fusion.3 = f32[2,32,2,34,16]{1,4,3,2,0:T(8,128)S(1)} fusion(f32[2,32,2,34,16]{1,4,3,2,0:T(8,128)S(1)} %slice-done, f32[2,32,1,34,16]{1,4,3,2,0:T(8,128)} %bitcast.220, f32[2,32,4,34,16]{1,4,3,2,0:T(8,128)S(1)} %copy-done.1), kind=kLoop, calls=%fused_computation.32 | loop fusion | flops 34816 | bytes 1253376 | tf_op jit(solution)/shard_map/scatter-add | solution.py:45
  24.4 1.2 %copy.89 = f32[2,32,1,544]{1,3,0,2:T(8,128)S(1)} copy(f32[2,32,1,544]{3,1,2,0:T(8,128)} %collective-permute-done.1) | data formatting | bytes 278528 | tf_op jit(solution)/shard_map/ppermute | solution.py:18
  29.9 0.8 select_bitcast_fusion.7
  31.8 0.7 fusion.15
  38.5 0.9 fusion.52
  39.3 0.9 copy.106
  40.3 0.9 maximum_bitcast_fusion.3
  41.8 0.8 reduce_sum.225
  42.6 1.4 %reduce_sum.228 = f32[32,16]{1,0:T(8,128)} reshape(f32[512]{0:T(512)} %get-tuple-element.105) | data formatting | bytes 4096 | tf_op jit(solution)/shard_map/reduce_sum | solution.py:126
  44.5 0.7 reduce_sum.229
  45.2 1.9 %copy.109 = f32[2,32,1,544]{3,1,2,0:T(8,128)} copy(f32[2,32,1,544]{1,3,2,0:T(8,128)} %get-tuple-element.116) | data formatting | bytes 278528 | tf_op jit(solution)/shard_map/slice | solution.py:16
  47.1 5.6 %collective-permute-start.5 = (f32[2,32,1,544]{3,1,2,0:T(8,128)}, f32[2,32,1,544]{3,1,2,0:T(8,128)}, u32[]{:S(2)}, u32[]{:S(2)}) collective-permute-start(f32[2,32,1,544]{3,1,2,0:T(8,128)} %copy.109), channel_id=1, source_target_pairs={{2,0},{4,2},{6,4},{8,6},{10,8},{12,10},{14,12},{16,14},{18,16},{20... | collective-permute-start | bytes 417800 | tf_op jit(solution)/shard_map/ppermute | solution.py:18
  52.7 1.9 %copy.107 = f32[2,32,1,544]{1,3,0,2:T(8,128)} copy(f32[2,32,1,544]{3,1,2,0:T(8,128)} %collective-permute-done.4) | data formatting | bytes 278528 | tf_op jit(solution)/shard_map/ppermute | solution.py:17
  54.6 1.1 %fusion.1 = f32[2,32,2,34,16]{1,4,3,2,0:T(8,128)S(1)} fusion(f32[2,32,2,34,16]{1,4,3,2,0:T(8,128)S(1)} %slice.539, f32[2,32,1,34,16]{1,4,3,2,0:T(8,128)} %bitcast.221, f32[2,32,4,34,16]{1,4,3,2,0:T(8,128)S(1)} %pad_add_fusion), kind=kLoop, calls=%fused_computation.28 | loop fusion | flops 34816 | bytes 1253376 | tf_op jit(solution)/shard_map/scatter-add | solution.py:45
  55.8 1.0 collective-permute-done.5
  56.7 1.1 %copy.110 = f32[2,32,1,544]{1,3,0,2:T(8,128)S(1)} copy(f32[2,32,1,544]{3,1,2,0:T(8,128)} %collective-permute-done.5) | data formatting | bytes 278528 | tf_op jit(solution)/shard_map/ppermute | solution.py:18
  62.0 0.8 select_bitcast_fusion.3
  63.3 0.7 fusion.19
  65.8 0.9 copy.125
  66.8 40.4 %all-reduce.18 = (f32[1,2,16]{2,1,0:T(2,128)S(1)}, f32[1,2,16]{2,1,0:T(2,128)S(1)}) all-reduce(f32[1,2,16]{2,1,0:T(2,128)S(1)} %maximum_bitcast_fusion.5, f32[1,2,16]{2,1,0:T(2,128)S(1)} %maximum_bitcast_fusion.4), channel_id=1, replica_groups=mesh['gx'=16,'gy'=2] {'gx','gy'}, use_global_device_ids=true, to_apply=%region_25.26 | all-reduce | flops 64 | bytes 512 | tf_op jit(solution)/shard_map/psum | solution.py:128
  (171 shorter events, 21.2 us)
Async XLA Ops:
  0.6 2.1 %copy-start.12 = (f32[2,32,2,512]{3,2,1,0:T(2,128)S(1)}, f32[2,32,2,512]{3,2,1,0:T(2,128)}, u32[]{:S(2)}) copy-start(f32[2,32,2,512]{3,2,1,0:T(2,128)} %param.20) | copy-start | bytes 786436
  4.9 9.2 %copy-start = (f32[2,32,4,34,16]{1,4,3,2,0:T(8,128)}, f32[2,32,4,34,16]{1,4,3,2,0:T(8,128)S(1)}, u32[]{:S(2)}) copy-start(f32[2,32,4,34,16]{1,4,3,2,0:T(8,128)S(1)} %pad_add_fusion.1) | copy-start | bytes 1671172
  6.3 15.0 %collective-permute-start = (f32[2,32,1,544]{3,1,2,0:T(8,128)}, f32[2,32,1,544]{3,1,2,0:T(8,128)}, u32[]{:S(2)}, u32[]{:S(2)}) collective-permute-start(f32[2,32,1,544]{3,1,2,0:T(8,128)} %copy.85), channel_id=1, source_target_pairs={{0,2},{2,4},{4,6},{6,8},{8,10},{10,12},{12,14},{14,16},{16,18},{18... | collective-permute-start | bytes 417800 | tf_op jit(solution)/shard_map/ppermute | solution.py:17
  10.1 4.0 %copy-start.13 = (s32[2,32,2,512]{3,2,1,0:T(2,128)S(1)}, s32[2,32,2,512]{3,2,1,0:T(2,128)}, u32[]{:S(2)}) copy-start(s32[2,32,2,512]{3,2,1,0:T(2,128)} %param.22) | copy-start | bytes 786436
  10.1 14.3 %collective-permute-start.1 = (f32[2,32,1,544]{3,1,2,0:T(8,128)}, f32[2,32,1,544]{3,1,2,0:T(8,128)}, u32[]{:S(2)}, u32[]{:S(2)}) collective-permute-start(f32[2,32,1,544]{3,1,2,0:T(8,128)} %copy.88), channel_id=1, source_target_pairs={{2,0},{4,2},{6,4},{8,6},{10,8},{12,10},{14,12},{16,14},{18,16},{20... | collective-permute-start | bytes 417800 | tf_op jit(solution)/shard_map/ppermute | solution.py:18
  14.1 9.1 %copy-start.1 = (f32[2,32,4,34,16]{1,4,3,2,0:T(8,128)S(1)}, f32[2,32,4,34,16]{1,4,3,2,0:T(8,128)}, u32[]{:S(2)}) copy-start(f32[2,32,4,34,16]{1,4,3,2,0:T(8,128)} %copy-done) | copy-start | bytes 1671172
  14.1 9.1 %slice-start = ((f32[2,32,4,34,16]{1,4,3,2,0:T(8,128)}), f32[2,32,2,34,16]{1,4,3,2,0:T(8,128)S(1)}, s32[]{:S(2)}) async-start(f32[2,32,4,34,16]{1,4,3,2,0:T(8,128)} %copy-done), calls=%async_computation | async-start | bytes 2228224 | tf_op jit(solution)/shard_map/slice | solution.py:43
  24.4 1.5 %copy-start.18 = (s32[32,1,512]{2,1,0:T(1,128)S(1)}, s32[32,1,512]{2,1,0:T(1,128)}, u32[]{:S(2)}) copy-start(s32[32,1,512]{2,1,0:T(1,128)} %get-tuple-element.204) | copy-start | bytes 196612
  24.4 1.5 %copy-start.17 = (s32[32,1,512]{2,1,0:T(1,128)S(1)}, s32[32,1,512]{2,1,0:T(1,128)}, u32[]{:S(2)}) copy-start(s32[32,1,512]{2,1,0:T(1,128)} %get-tuple-element.205) | copy-start | bytes 196612
  24.4 1.5 %copy-start.16 = (s32[32,1,512]{2,1,0:T(1,128)S(1)}, s32[32,1,512]{2,1,0:T(1,128)}, u32[]{:S(2)}) copy-start(s32[32,1,512]{2,1,0:T(1,128)} %get-tuple-element.181) | copy-start | bytes 196612
  24.4 1.6 %copy-start.15 = (s32[32,1,512]{2,1,0:T(1,128)S(1)}, s32[32,1,512]{2,1,0:T(1,128)}, u32[]{:S(2)}) copy-start(s32[32,1,512]{2,1,0:T(1,128)} %get-tuple-element.180) | copy-start | bytes 196612
  25.8 1.3 %collective-permute-start.2 = (f32[2,32,1,32]{1,3,0,2:T(8,128)S(1)}, f32[2,32,1,32]{1,3,0,2:T(8,128)S(1)}, u32[]{:S(2)}, u32[]{:S(2)}) collective-permute-start(f32[2,32,1,32]{1,3,0,2:T(8,128)S(1)} %bitcast.267), channel_id=1, source_target_pairs={{0,1},{1,0},{2,3},{3,2},{4,5},{5,4},{6,7},{7,6},{8,9},{9,8},{10,11... | collective-permute-start | bytes 24584 | tf_op jit(solution)/shard_map/ppermute | solution.py:17
  26.1 1.4 %collective-permute-start.3 = (f32[2,32,1,32]{1,3,0,2:T(8,128)S(1)}, f32[2,32,1,32]{1,3,0,2:T(8,128)S(1)}, u32[]{:S(2)}, u32[]{:S(2)}) collective-permute-start(f32[2,32,1,32]{1,3,0,2:T(8,128)S(1)} %bitcast.266), channel_id=1, source_target_pairs={{1,0},{0,1},{3,2},{2,3},{5,4},{4,5},{7,6},{6,7},{9,8},{8,9},{11,10... | collective-permute-start | bytes 24584 | tf_op jit(solution)/shard_map/ppermute | solution.py:18
  30.8 4.4 %copy-start.9 = (pred[1,32,2,512]{1,3,2,0:T(8,128)(4,1)S(1)}, pred[1,32,2,512]{1,3,2,0:T(8,128)(4,1)}, u32[]{:S(2)}) copy-start(pred[1,32,2,512]{1,3,2,0:T(8,128)(4,1)} %get-tuple-element.148) | copy-start | bytes 98308
  30.8 4.4 %copy-start.10 = (pred[1,32,2,512]{1,3,2,0:T(8,128)(4,1)S(1)}, pred[1,32,2,512]{1,3,2,0:T(8,128)(4,1)}, u32[]{:S(2)}) copy-start(pred[1,32,2,512]{1,3,2,0:T(8,128)(4,1)} %get-tuple-element.155) | copy-start | bytes 98308
  30.8 4.4 %copy-start.11 = (pred[1,32,2,512]{1,3,2,0:T(8,128)(4,1)S(1)}, pred[1,32,2,512]{1,3,2,0:T(8,128)(4,1)}, u32[]{:S(2)}) copy-start(pred[1,32,2,512]{1,3,2,0:T(8,128)(4,1)} %get-tuple-element.156) | copy-start | bytes 98308
  34.6 1.0 copy-start.2
  35.2 0.9 copy-start.6
  35.2 1.0 copy-start.7
  35.2 1.0 copy-start.8
  36.2 0.9 copy-start.3
  36.3 1.0 copy-start.4
  36.3 1.0 copy-start.5
  38.4 1.9 %copy-start.14 = (f32[1,32,512]{2,1,0:T(8,128)S(1)}, f32[1,32,512]{2,1,0:T(8,128)}, u32[]{:S(2)}) copy-start(f32[1,32,512]{2,1,0:T(8,128)} %get-tuple-element.192) | copy-start | bytes 196612
  40.2 12.5 %collective-permute-start.4 = (f32[2,32,1,544]{3,1,2,0:T(8,128)}, f32[2,32,1,544]{3,1,2,0:T(8,128)}, u32[]{:S(2)}, u32[]{:S(2)}) collective-permute-start(f32[2,32,1,544]{3,1,2,0:T(8,128)} %copy.106), channel_id=1, source_target_pairs={{0,2},{2,4},{4,6},{6,8},{8,10},{10,12},{12,14},{14,16},{16,18},{18... | collective-permute-start | bytes 417800 | tf_op jit(solution)/shard_map/ppermute | solution.py:17
  47.1 9.6 %collective-permute-start.5 = (f32[2,32,1,544]{3,1,2,0:T(8,128)}, f32[2,32,1,544]{3,1,2,0:T(8,128)}, u32[]{:S(2)}, u32[]{:S(2)}) collective-permute-start(f32[2,32,1,544]{3,1,2,0:T(8,128)} %copy.109), channel_id=1, source_target_pairs={{2,0},{4,2},{6,4},{8,6},{10,8},{12,10},{14,12},{16,14},{18,16},{20... | collective-permute-start | bytes 417800 | tf_op jit(solution)/shard_map/ppermute | solution.py:18
  54.6 3.5 %copy-start.19 = (f32[16]{0:T(128)S(1)}, f32[16]{0:T(128)}, u32[]{:S(2)}) copy-start(f32[16]{0:T(128)} %reduce_sum.226) | copy-start | bytes 196
  58.0 1.3 %collective-permute-start.6 = (f32[2,32,1,32]{1,3,0,2:T(8,128)S(1)}, f32[2,32,1,32]{1,3,0,2:T(8,128)S(1)}, u32[]{:S(2)}, u32[]{:S(2)}) collective-permute-start(f32[2,32,1,32]{1,3,0,2:T(8,128)S(1)} %bitcast.269), channel_id=1, source_target_pairs={{0,1},{1,0},{2,3},{3,2},{4,5},{5,4},{6,7},{7,6},{8,9},{9,8},{10,11... | collective-permute-start | bytes 24584 | tf_op jit(solution)/shard_map/ppermute | solution.py:17
  58.2 1.4 %collective-permute-start.7 = (f32[2,32,1,32]{1,3,0,2:T(8,128)S(1)}, f32[2,32,1,32]{1,3,0,2:T(8,128)S(1)}, u32[]{:S(2)}, u32[]{:S(2)}) collective-permute-start(f32[2,32,1,32]{1,3,0,2:T(8,128)S(1)} %bitcast.268), channel_id=1, source_target_pairs={{1,0},{0,1},{3,2},{2,3},{5,4},{4,5},{7,6},{6,7},{9,8},{8,9},{11,10... | collective-permute-start | bytes 24584 | tf_op jit(solution)/shard_map/ppermute | solution.py:18
where the time goes:
time: 108 us
  blocking collectives  40.4 us (37%)
  local copies, waits for them, and re-layouts  25.6 us (24%)
  other arithmetic  23.8 us (22%)
  starting transfers between devices  13.8 us (13%)
  waiting for transfers between devices  2.67 us (2%)
  between operations  1.49 us (1%)
    psum x1, blocking collectives, shards(): totals.append(lax.psum(terms, ('gx', 'gy')))  40.4 us
    ppermute x4, starting transfers between devices, padded(): after = lax.ppermute(leading, axis, down)  10.7 us
    unnamed x48, local copies, waits for them, and re-layouts  3.88 us
    ppermute x2, local copies, waits for them, and re-layouts, padded(): before = lax.ppermute(last, axis, up)  3.87 us
    slice x4, local copies, waits for them, and re-layouts, padded(): leading = lax.slice_in_dim(array, 0, width, axis=dim)  3.72 us
    eq x2, other arithmetic, spread(): chosen = jnp.where((codes == direction)[None], state, jnp.zeros_like(state))  3.36 us
    ppermute x4, starting transfers between devices, padded(): before = lax.ppermute(last, axis, up)  3.11 us
    scatter-add x4, other arithmetic, settle(): middle = extended[:, :, 1:cols + 1].at[:, :, 0].add(got[:, :, 0]).at[:, :...  2.53 us
  transfers between devices with their start and end apart: 8, of which 5 were waited for; matrix products, arithmetic and copies ran while one was open for 20% of the time, Pallas kernels for 0%

commit v1 on v0

--- a/solution.py
+++ b/solution.py
@@ -125,7 +125,7 @@
         count_sum = jnp.sum(state[0], axis=(0, 1, 2))
         liquid_sum = jnp.sum(state[0] * state[1], axis=(0, 1, 2))
         terms = jnp.stack([count_sum, liquid_sum])
-        totals.append(lax.psum(terms, ("gx", "gy")))
+        totals.append(lax.psum(lax.psum(terms, "gy"), "gx"))
     summed = jnp.stack(totals)
     cells_x = cols * lax.axis_size("gx")
     cells_y = rows * lax.axis_size("gy")

time: 108 us -> 113 us (1.046)
  blocking collectives: 40.4 us -> 45.1 us
    psum x1 -> x2, blocking collectives: 40.4 us -> 45.1 us  [shards(): totals.append(lax.psum(lax.psum(terms, 'gy'), 'gx'))]
  transfers between devices with their start and end apart: 8 -> 8, of which waited for: 5 -> 5; matrix products, arithmetic and copies ran while one was open for 20% -> 19% of each run, Pallas kernels for 0% -> 0%
where the time goes in v1:
time: 113 us; the launch traced here: 112 us
  blocking collectives  45.1 us (40%)
  local copies, waits for them, and re-layouts  25.6 us (23%)
  other arithmetic  23.8 us (21%)
  starting transfers between devices  13.8 us (12%)
  waiting for transfers between devices  2.67 us (2%)
  between operations  1.49 us (1%)
    psum x2, blocking collectives, shards(): totals.append(lax.psum(lax.psum(terms, 'gy'), 'gx'))  45.1 us
    ppermute x4, starting transfers between devices, padded(): after = lax.ppermute(leading, axis, down)  10.7 us
    unnamed x48, local copies, waits for them, and re-layouts  3.88 us
    ppermute x2, local copies, waits for them, and re-layouts, padded(): before = lax.ppermute(last, axis, up)  3.87 us
    slice x4, local copies, waits for them, and re-layouts, padded(): leading = lax.slice_in_dim(array, 0, width, axis=dim)  3.72 us
    eq x2, other arithmetic, spread(): chosen = jnp.where((codes == direction)[None], state, jnp.zeros_like(state))  3.36 us
    ppermute x4, starting transfers between devices, padded(): before = lax.ppermute(last, axis, up)  3.11 us
    scatter-add x4, other arithmetic, settle(): middle = extended[:, :, 1:cols + 1].at[:, :, 0].add(got[:, :, 0]).at[:, :...  2.53 us
  transfers between devices with their start and end apart: 8, of which 5 were waited for; matrix products, arithmetic and copies ran while one was open for 19% of the time, Pallas kernels for 0%

profile of v1, /device:TPU:0, one launch (start us, length us, event | category | flops | bytes accessed | tf_op | source)
XLA Modules:
  0.0 112.4 jit_solution(3750869834975199675)
XLA Ops:
  0.6 1.0 fusion.55
  1.9 0.8 broadcast_compare_fusion.16
  3.1 1.2 %broadcast_select_fusion.17 = (f32[2,32,2,32,16]{1,4,3,2,0:T(8,128)S(1)}, f32[2,32,2,32,16]{1,4,3,2,0:T(8,128)S(1)}, f32[2,32,2,32,16]{1,4,3,2,0:T(8,128)S(1)}, ...) fusion(f32[2,32,2,32,16]{1,4,3,2,0:T(8,128)S(1)} %bitcast.217, ...), kind=kLoop, calls=%fused_computation.50 | loop fusion | flops 589824 | bytes 2916352 | tf_op jit(solution)/shard_map/jit(_where)/select_n | solution.py:29
  5.2 1.1 copy.85
  6.3 3.0 %collective-permute-start = (f32[2,32,1,544]{3,1,2,0:T(8,128)}, f32[2,32,1,544]{3,1,2,0:T(8,128)}, u32[]{:S(2)}, u32[]{:S(2)}) collective-permute-start(f32[2,32,1,544]{3,1,2,0:T(8,128)} %copy.85), channel_id=1, source_target_pairs={{0,2},{2,4},{4,6},{6,8},{8,10},{10,12},{12,14},{14,16},{16,18},{18... | collective-permute-start | bytes 417800 | tf_op jit(solution)/shard_map/ppermute | solution.py:17
  9.2 0.9 copy.88
  10.1 4.0 %collective-permute-start.1 = (f32[2,32,1,544]{3,1,2,0:T(8,128)}, f32[2,32,1,544]{3,1,2,0:T(8,128)}, u32[]{:S(2)}, u32[]{:S(2)}) collective-permute-start(f32[2,32,1,544]{3,1,2,0:T(8,128)} %copy.88), channel_id=1, source_target_pairs={{2,0},{4,2},{6,4},{8,6},{10,8},{12,10},{14,12},{16,14},{18,16},{20... | collective-permute-start | bytes 417800 | tf_op jit(solution)/shard_map/ppermute | solution.py:18
  14.8 1.0 copy.130
  15.9 2.5 %broadcast_compare_fusion.17 = (pred[1,32,2,512]{1,3,2,0:T(8,128)(4,1)}, pred[1,32,2,512]{1,3,2,0:T(8,128)(4,1)}, pred[1,32,2,512]{1,3,2,0:T(8,128)(4,1)}, pred[...) fusion(s32[1,32,2,512]{1,3,2,0:T(8,128)} %copy.130), kind=kLoop, calls=%fused_computation.87 | loop fusion | flops 294912 | bytes 425984 | tf_op jit(solution)/shard_map/eq | solution.py:29
  18.4 2.0 %fusion.56 = (s32[32,1,512]{2,1,0:T(1,128)}, s32[32,1,512]{2,1,0:T(1,128)}, s32[32,1,512]{2,1,0:T(1,128)}, s32[32,1,512]{2,1,0:T(1,128)}) fusion(s32[32,2,512]{2,1,0:T(2,128)} %get-tuple-element.168, s32[32,2,512]{2,1,0:T(2,128)} %get-tuple-element.169), kind=kLoop, calls=%fused_computation.232 | loop fusion | bytes 524288 | tf_op jit(solution)/shard_map/slice | solution.py:109
  20.4 0.9 fusion.57
  21.3 1.9 %copy.86 = f32[2,32,1,544]{1,3,0,2:T(8,128)} copy(f32[2,32,1,544]{3,1,2,0:T(8,128)} %collective-permute-done) | data formatting | bytes 278528 | tf_op jit(solution)/shard_map/ppermute | solution.py:17
  23.3 1.1 %fusion.3 = f32[2,32,2,34,16]{1,4,3,2,0:T(8,128)S(1)} fusion(f32[2,32,2,34,16]{1,4,3,2,0:T(8,128)S(1)} %slice-done, f32[2,32,1,34,16]{1,4,3,2,0:T(8,128)} %bitcast.218, f32[2,32,4,34,16]{1,4,3,2,0:T(8,128)S(1)} %copy-done.1), kind=kLoop, calls=%fused_computation.32 | loop fusion | flops 34816 | bytes 1253376 | tf_op jit(solution)/shard_map/scatter-add | solution.py:45
  24.4 1.2 %copy.89 = f32[2,32,1,544]{1,3,0,2:T(8,128)S(1)} copy(f32[2,32,1,544]{3,1,2,0:T(8,128)} %collective-permute-done.1) | data formatting | bytes 278528 | tf_op jit(solution)/shard_map/ppermute | solution.py:18
  29.9 0.8 select_bitcast_fusion.7
  31.8 0.7 fusion.15
  38.5 0.9 fusion.52
  39.3 0.9 copy.106
  40.3 0.9 maximum_bitcast_fusion.3
  41.8 0.8 reduce_sum.225
  42.6 1.4 %reduce_sum.228 = f32[32,16]{1,0:T(8,128)} reshape(f32[512]{0:T(512)} %get-tuple-element.105) | data formatting | bytes 4096 | tf_op jit(solution)/shard_map/reduce_sum | solution.py:126
  45.2 1.9 %copy.109 = f32[2,32,1,544]{3,1,2,0:T(8,128)} copy(f32[2,32,1,544]{1,3,2,0:T(8,128)} %get-tuple-element.118) | data formatting | bytes 278528 | tf_op jit(solution)/shard_map/slice | solution.py:16
  47.1 5.6 %collective-permute-start.5 = (f32[2,32,1,544]{3,1,2,0:T(8,128)}, f32[2,32,1,544]{3,1,2,0:T(8,128)}, u32[]{:S(2)}, u32[]{:S(2)}) collective-permute-start(f32[2,32,1,544]{3,1,2,0:T(8,128)} %copy.109), channel_id=1, source_target_pairs={{2,0},{4,2},{6,4},{8,6},{10,8},{12,10},{14,12},{16,14},{18,16},{20... | collective-permute-start | bytes 417800 | tf_op jit(solution)/shard_map/ppermute | solution.py:18
  52.7 1.9 %copy.107 = f32[2,32,1,544]{1,3,0,2:T(8,128)} copy(f32[2,32,1,544]{3,1,2,0:T(8,128)} %collective-permute-done.4) | data formatting | bytes 278528 | tf_op jit(solution)/shard_map/ppermute | solution.py:17
  54.6 1.1 %fusion.1 = f32[2,32,2,34,16]{1,4,3,2,0:T(8,128)S(1)} fusion(f32[2,32,2,34,16]{1,4,3,2,0:T(8,128)S(1)} %slice.539, f32[2,32,1,34,16]{1,4,3,2,0:T(8,128)} %bitcast.219, f32[2,32,4,34,16]{1,4,3,2,0:T(8,128)S(1)} %pad_add_fusion), kind=kLoop, calls=%fused_computation.28 | loop fusion | flops 34816 | bytes 1253376 | tf_op jit(solution)/shard_map/scatter-add | solution.py:45
  55.8 1.0 collective-permute-done.5
  56.7 1.1 copy.110
  62.0 0.8 select_bitcast_fusion.3
  63.3 0.7 fusion.19
  65.8 0.9 copy.125
  66.8 2.5 %all-reduce.19 = (f32[2,16]{1,0:T(2,128)S(1)}, f32[2,16]{1,0:T(2,128)S(1)}) all-reduce(f32[2,16]{1,0:T(2,128)S(1)} %pad_maximum_fusion.9, f32[2,16]{1,0:T(2,128)S(1)} %pad_maximum_fusion.8), channel_id=1, replica_groups=mesh['gx'=16,'gy'=2] {'gy'}, use_global_device_ids=true, to_apply=%region_26.27 | all-reduce | flops 64 | bytes 512 | tf_op jit(solution)/shard_map/psum | solution.py:128
  69.2 42.6 %all-reduce.18 = (f32[1,2,16]{2,1,0:T(2,128)S(1)}, f32[1,2,16]{2,1,0:T(2,128)S(1)}) all-reduce(f32[1,2,16]{2,1,0:T(2,128)S(1)} %bitcast.272, f32[1,2,16]{2,1,0:T(2,128)S(1)} %bitcast.273), channel_id=1, replica_groups=mesh['gx'=16,'gy'=2] {'gx'}, use_global_device_ids=true, to_apply=%region_27.28 | all-reduce | flops 64 | bytes 512 | tf_op jit(solution)/shard_map/psum | solution.py:128
  (172 shorter events, 21.9 us)
Async XLA Ops:
  0.6 2.1 %copy-start.12 = (f32[2,32,2,512]{3,2,1,0:T(2,128)S(1)}, f32[2,32,2,512]{3,2,1,0:T(2,128)}, u32[]{:S(2)}) copy-start(f32[2,32,2,512]{3,2,1,0:T(2,128)} %param.20) | copy-start | bytes 786436
  4.9 9.2 %copy-start = (f32[2,32,4,34,16]{1,4,3,2,0:T(8,128)}, f32[2,32,4,34,16]{1,4,3,2,0:T(8,128)S(1)}, u32[]{:S(2)}) copy-start(f32[2,32,4,34,16]{1,4,3,2,0:T(8,128)S(1)} %pad_add_fusion.1) | copy-start | bytes 1671172
  6.3 15.0 %collective-permute-start = (f32[2,32,1,544]{3,1,2,0:T(8,128)}, f32[2,32,1,544]{3,1,2,0:T(8,128)}, u32[]{:S(2)}, u32[]{:S(2)}) collective-permute-start(f32[2,32,1,544]{3,1,2,0:T(8,128)} %copy.85), channel_id=1, source_target_pairs={{0,2},{2,4},{4,6},{6,8},{8,10},{10,12},{12,14},{14,16},{16,18},{18... | collective-permute-start | bytes 417800 | tf_op jit(solution)/shard_map/ppermute | solution.py:17
  10.1 4.0 %copy-start.13 = (s32[2,32,2,512]{3,2,1,0:T(2,128)S(1)}, s32[2,32,2,512]{3,2,1,0:T(2,128)}, u32[]{:S(2)}) copy-start(s32[2,32,2,512]{3,2,1,0:T(2,128)} %param.22) | copy-start | bytes 786436
  10.1 14.3 %collective-permute-start.1 = (f32[2,32,1,544]{3,1,2,0:T(8,128)}, f32[2,32,1,544]{3,1,2,0:T(8,128)}, u32[]{:S(2)}, u32[]{:S(2)}) collective-permute-start(f32[2,32,1,544]{3,1,2,0:T(8,128)} %copy.88), channel_id=1, source_target_pairs={{2,0},{4,2},{6,4},{8,6},{10,8},{12,10},{14,12},{16,14},{18,16},{20... | collective-permute-start | bytes 417800 | tf_op jit(solution)/shard_map/ppermute | solution.py:18
  14.1 9.1 %copy-start.1 = (f32[2,32,4,34,16]{1,4,3,2,0:T(8,128)S(1)}, f32[2,32,4,34,16]{1,4,3,2,0:T(8,128)}, u32[]{:S(2)}) copy-start(f32[2,32,4,34,16]{1,4,3,2,0:T(8,128)} %copy-done) | copy-start | bytes 1671172
  14.1 9.1 %slice-start = ((f32[2,32,4,34,16]{1,4,3,2,0:T(8,128)}), f32[2,32,2,34,16]{1,4,3,2,0:T(8,128)S(1)}, s32[]{:S(2)}) async-start(f32[2,32,4,34,16]{1,4,3,2,0:T(8,128)} %copy-done), calls=%async_computation | async-start | bytes 2228224 | tf_op jit(solution)/shard_map/slice | solution.py:43
  24.4 1.5 %copy-start.18 = (s32[32,1,512]{2,1,0:T(1,128)S(1)}, s32[32,1,512]{2,1,0:T(1,128)}, u32[]{:S(2)}) copy-start(s32[32,1,512]{2,1,0:T(1,128)} %get-tuple-element.206) | copy-start | bytes 196612
  24.4 1.5 %copy-start.17 = (s32[32,1,512]{2,1,0:T(1,128)S(1)}, s32[32,1,512]{2,1,0:T(1,128)}, u32[]{:S(2)}) copy-start(s32[32,1,512]{2,1,0:T(1,128)} %get-tuple-element.207) | copy-start | bytes 196612
  24.4 1.5 %copy-start.16 = (s32[32,1,512]{2,1,0:T(1,128)S(1)}, s32[32,1,512]{2,1,0:T(1,128)}, u32[]{:S(2)}) copy-start(s32[32,1,512]{2,1,0:T(1,128)} %get-tuple-element.183) | copy-start | bytes 196612
  24.4 1.6 %copy-start.15 = (s32[32,1,512]{2,1,0:T(1,128)S(1)}, s32[32,1,512]{2,1,0:T(1,128)}, u32[]{:S(2)}) copy-start(s32[32,1,512]{2,1,0:T(1,128)} %get-tuple-element.182) | copy-start | bytes 196612
  25.8 1.3 %collective-permute-start.2 = (f32[2,32,1,32]{1,3,0,2:T(8,128)S(1)}, f32[2,32,1,32]{1,3,0,2:T(8,128)S(1)}, u32[]{:S(2)}, u32[]{:S(2)}) collective-permute-start(f32[2,32,1,32]{1,3,0,2:T(8,128)S(1)} %bitcast.265), channel_id=1, source_target_pairs={{0,1},{1,0},{2,3},{3,2},{4,5},{5,4},{6,7},{7,6},{8,9},{9,8},{10,11... | collective-permute-start | bytes 24584 | tf_op jit(solution)/shard_map/ppermute | solution.py:17
  26.1 1.4 %collective-permute-start.3 = (f32[2,32,1,32]{1,3,0,2:T(8,128)S(1)}, f32[2,32,1,32]{1,3,0,2:T(8,128)S(1)}, u32[]{:S(2)}, u32[]{:S(2)}) collective-permute-start(f32[2,32,1,32]{1,3,0,2:T(8,128)S(1)} %bitcast.264), channel_id=1, source_target_pairs={{1,0},{0,1},{3,2},{2,3},{5,4},{4,5},{7,6},{6,7},{9,8},{8,9},{11,10... | collective-permute-start | bytes 24584 | tf_op jit(solution)/shard_map/ppermute | solution.py:18
  30.8 4.4 %copy-start.9 = (pred[1,32,2,512]{1,3,2,0:T(8,128)(4,1)S(1)}, pred[1,32,2,512]{1,3,2,0:T(8,128)(4,1)}, u32[]{:S(2)}) copy-start(pred[1,32,2,512]{1,3,2,0:T(8,128)(4,1)} %get-tuple-element.150) | copy-start | bytes 98308
  30.8 4.4 %copy-start.10 = (pred[1,32,2,512]{1,3,2,0:T(8,128)(4,1)S(1)}, pred[1,32,2,512]{1,3,2,0:T(8,128)(4,1)}, u32[]{:S(2)}) copy-start(pred[1,32,2,512]{1,3,2,0:T(8,128)(4,1)} %get-tuple-element.157) | copy-start | bytes 98308
  30.8 4.4 %copy-start.11 = (pred[1,32,2,512]{1,3,2,0:T(8,128)(4,1)S(1)}, pred[1,32,2,512]{1,3,2,0:T(8,128)(4,1)}, u32[]{:S(2)}) copy-start(pred[1,32,2,512]{1,3,2,0:T(8,128)(4,1)} %get-tuple-element.158) | copy-start | bytes 98308
  34.6 1.0 copy-start.2
  35.2 0.9 copy-start.6
  35.2 1.0 copy-start.7
  35.2 1.0 copy-start.8
  36.2 0.9 copy-start.3
  36.3 1.0 copy-start.4
  36.3 1.0 copy-start.5
  38.4 1.9 %copy-start.14 = (f32[1,32,512]{2,1,0:T(8,128)S(1)}, f32[1,32,512]{2,1,0:T(8,128)}, u32[]{:S(2)}) copy-start(f32[1,32,512]{2,1,0:T(8,128)} %get-tuple-element.194) | copy-start | bytes 196612
  40.2 12.5 %collective-permute-start.4 = (f32[2,32,1,544]{3,1,2,0:T(8,128)}, f32[2,32,1,544]{3,1,2,0:T(8,128)}, u32[]{:S(2)}, u32[]{:S(2)}) collective-permute-start(f32[2,32,1,544]{3,1,2,0:T(8,128)} %copy.106), channel_id=1, source_target_pairs={{0,2},{2,4},{4,6},{6,8},{8,10},{10,12},{12,14},{14,16},{16,18},{18... | collective-permute-start | bytes 417800 | tf_op jit(solution)/shard_map/ppermute | solution.py:17
  47.1 9.6 %collective-permute-start.5 = (f32[2,32,1,544]{3,1,2,0:T(8,128)}, f32[2,32,1,544]{3,1,2,0:T(8,128)}, u32[]{:S(2)}, u32[]{:S(2)}) collective-permute-start(f32[2,32,1,544]{3,1,2,0:T(8,128)} %copy.109), channel_id=1, source_target_pairs={{2,0},{4,2},{6,4},{8,6},{10,8},{12,10},{14,12},{16,14},{18,16},{20... | collective-permute-start | bytes 417800 | tf_op jit(solution)/shard_map/ppermute | solution.py:18
  54.6 3.5 %copy-start.19 = (f32[16]{0:T(128)S(1)}, f32[16]{0:T(128)}, u32[]{:S(2)}) copy-start(f32[16]{0:T(128)} %reduce_sum.226) | copy-start | bytes 196
  58.0 1.3 %collective-permute-start.6 = (f32[2,32,1,32]{1,3,0,2:T(8,128)S(1)}, f32[2,32,1,32]{1,3,0,2:T(8,128)S(1)}, u32[]{:S(2)}, u32[]{:S(2)}) collective-permute-start(f32[2,32,1,32]{1,3,0,2:T(8,128)S(1)} %bitcast.267), channel_id=1, source_target_pairs={{0,1},{1,0},{2,3},{3,2},{4,5},{5,4},{6,7},{7,6},{8,9},{9,8},{10,11... | collective-permute-start | bytes 24584 | tf_op jit(solution)/shard_map/ppermute | solution.py:17
  58.2 1.4 %collective-permute-start.7 = (f32[2,32,1,32]{1,3,0,2:T(8,128)S(1)}, f32[2,32,1,32]{1,3,0,2:T(8,128)S(1)}, u32[]{:S(2)}, u32[]{:S(2)}) collective-permute-start(f32[2,32,1,32]{1,3,0,2:T(8,128)S(1)} %bitcast.266), channel_id=1, source_target_pairs={{1,0},{0,1},{3,2},{2,3},{5,4},{4,5},{7,6},{6,7},{9,8},{8,9},{11,10... | collective-permute-start | bytes 24584 | tf_op jit(solution)/shard_map/ppermute | solution.py:18
